TPU v7x, 32 devices: a whole 2x2x4 slice. The times are simulated.
32 devices in a mesh: dp: 8 (over z, y), mp: 4 (over x, core).
Axes of the slice: x: 2, y: 2, z: 4, core: 2. Of those that a mesh axis runs over, the one named last changes fastest.
Arguments:
- picture_skip_activations: bfloat16 [16384, 1152], P('dp'), as said below
- caption_closing_activations: bfloat16 [64, 1152], P('dp'), as said below
- normaliser_multipliers: float32 [3, 1152], replicated, may hold values from 0.1 to 1.9
- widening_matrix: bfloat16 [1152, 4304], P('dp', 'mp'), may hold values from -0.1875 to 0.1875
- contracting_matrix: bfloat16 [4304, 1152], P('mp', 'dp'), as said below
- caption_mapping_matrix: bfloat16 [1152, 1152], replicated, as said below
- sharpness_factor: float32 [1], replicated, may hold values from 8 to 32
- score_offset_term: float32 [1], replicated, may hold values from -8 to -3
Outputs:
- row_loss: float32 [64], P('dp')
- col_loss: float32 [64], P('dp')
Inputs may be any that keep to these rules, and one draw needn't show every extreme that they name: `picture_skip_activations`: entries lie within -8 and 8. `caption_closing_activations`: entries lie within -8 and 8. `contracting_matrix`: entries are at most 4.4 / sqrt(4304) in magnitude. `caption_mapping_matrix`: diagonal entries lie within 1 - 2.1 / sqrt(1152) and 1 + 2.1 / sqrt(1152), the others within -2.1 / sqrt(1152) and 2.1 / sqrt(1152).
All inputs are finite; a program needn't handle non-finite values.
Results may differ from a plain program's by a relative error of at most 0.01.
Values may be sent and summed in bfloat16 or wider, within the bound.
A program may use at most 128 MiB of HBM per device.

v0:
```python
import jax
import jax.numpy as jnp
from jax import lax
from jax.sharding import PartitionSpec as P

PATCHES = 256


def layer_norm(values, norm_gain):
    average = jnp.mean(values, axis=-1, keepdims=True)
    centred = values - average
    spread = jnp.mean(centred * centred, axis=-1, keepdims=True)
    return centred * lax.rsqrt(spread + 1e-06) * norm_gain


def unit_vector(vector):
    length = jnp.sqrt(jnp.sum(vector * vector, axis=-1, keepdims=True))
    return (vector / jnp.maximum(length, 1.0)).astype(jnp.bfloat16)


def pool_images(image_final):
    return jnp.mean(image_final.reshape(-1, PATCHES, image_final.shape[1]), axis=1)


def on_device(
    picture_skip_activations,
    caption_closing_activations,
    normaliser_multipliers,
    widening_matrix,
    contracting_matrix,
    caption_mapping_matrix,
    sharpness_factor,
    score_offset_term,
):
    image_rows = picture_skip_activations.astype(jnp.float32)
    image_normed = layer_norm(image_rows, normaliser_multipliers[0]).astype(jnp.bfloat16)
    inner_weight = lax.all_gather(widening_matrix, "dp", axis=0, tiled=True)
    image_units = jax.nn.gelu(
        jnp.dot(image_normed, inner_weight, preferred_element_type=jnp.float32), approximate=True
    ).astype(jnp.bfloat16)
    partial_out = jnp.dot(
        image_units,
        lax.all_gather(contracting_matrix, "dp", axis=1, tiled=True),
        preferred_element_type=jnp.float32,
    )
    unit_share = lax.psum_scatter(
        partial_out.astype(jnp.bfloat16), "mp", scatter_dimension=0, tiled=True
    ).astype(jnp.float32)
    own_count = unit_share.shape[0]
    own_first = lax.axis_index("mp") * own_count
    own_rows = lax.dynamic_slice_in_dim(image_rows, own_first, own_count, 0)
    image_final = layer_norm(own_rows + unit_share, normaliser_multipliers[1])
    own_emb = unit_vector(pool_images(image_final))
    picture_code_direction = lax.all_gather(own_emb, "mp", axis=0, tiled=True)
    text_normed = layer_norm(
        caption_closing_activations.astype(jnp.float32), normaliser_multipliers[2]
    ).astype(jnp.bfloat16)
    text_vector = jnp.dot(text_normed, caption_mapping_matrix, preferred_element_type=jnp.float32)
    caption_code_direction = unit_vector(text_vector)
    offset = lax.axis_index("dp") * picture_code_direction.shape[0]
    matching_scores = (
        sharpness_factor[0]
        * jnp.einsum(
            "pe,qe->pq",
            picture_code_direction,
            lax.all_gather(caption_code_direction, "dp", axis=0, tiled=True),
            preferred_element_type=jnp.float32,
        )
        + score_offset_term[0]
    )
    row_index = offset + lax.broadcasted_iota(jnp.int32, matching_scores.shape, 0)
    col_index = lax.broadcasted_iota(jnp.int32, matching_scores.shape, 1)
    labels = jnp.where(row_index == col_index, 1.0, -1.0).astype(jnp.float32)
    loss_terms = jax.nn.softplus(-labels * matching_scores)
    row_loss = jnp.sum(loss_terms, axis=1)
    col_loss = lax.psum_scatter(jnp.sum(loss_terms, axis=0), "dp", scatter_dimension=0, tiled=True)
    return (row_loss, col_loss)


def solution(mesh):
    return jax.shard_map(
        on_device,
        mesh=mesh,
        in_specs=(P("dp", None), P("dp", None), P(), P("dp", "mp"), P("mp", "dp"), P(), P(), P()),
        out_specs=(P("dp"), P("dp")),
        check_vma=False,
    )
```

profile of v0, /device:TPU:0, one launch (start us, length us, event | category | flops | bytes accessed | tf_op | source)
XLA Modules:
  0.0 232.3 jit_solution(16782825262965968562)
XLA Ops:
  7.2 0.7 all-gather.4.cloned.1.call-update
  8.0 0.7 all-gather.6.cloned.1.call-update
  8.7 0.9 slice_reduce_fusion
  9.7 3.2 %convert_reduce_fusion = f32[2048]{0:T(1024)S(1)} fusion(bf16[2048,1152]{1,0:T(8,128)(2,1)} %param.8), kind=kLoop, calls=%fused_computation.12 | loop fusion | flops 4716544 | bytes 4726784 | tf_op jit(solution)/shard_map/reduce_sum | solution.py:10
  12.9 1.4 multiply_reduce_fusion
  14.3 53.6 %all-gather.4.cloned.1.call-done = bf16[1152,1076]{1,0:T(8,128)(2,1)} async-done(((bf16[144,1076]{1,0:T(8,128)(2,1)}), bf16[1152,1076]{1,0:T(8,128)(2,1)}) %all-gather.4.cloned.1.call-update) | async-done | bytes 2479120 | tf_op jit(solution)/shard_map/all_gather | solution.py:37
  67.9 55.8 %all-gather.6.cloned.1.call-done = bf16[1076,1152]{0,1:T(8,128)(2,1)} async-done(((bf16[1076,144]{0,1:T(8,128)(2,1)}), bf16[1076,1152]{0,1:T(8,128)(2,1)}) %all-gather.6.cloned.1.call-update) | async-done | bytes 2479120 | tf_op jit(solution)/shard_map/all_gather | solution.py:43
  123.7 20.0 %convolution_convert_fusion = bf16[2048,1152]{1,0:T(8,128)(2,1)} fusion(bf16[1076,1152]{0,1:T(8,128)(2,1)} %all-gather.6.cloned.1.call-done, bf16[1152,1076]{1,0:T(8,128)(2,1)} %all-gather.4.cloned.1.call-done, bf16[2048,1152]{1,0:T(8,128)(2,1)} %param.8, f32[1152]{0:T(1024)S(1)} %get-tuple-element.3, f32[2048]{0:T(1024)S(1)} %add_rsqrt_fusion, ...), kind=kOutput, calls=%fused_computation.11 | convolution fusion | flops 10188398592 | bytes 14416384 | tf_op jit(solution)/shard_map/dot_general | solution.py:41
  143.8 7.9 %convert_element_type.27 = f32[2048,1152]{1,0:T(8,128)} convert(bf16[2048,1152]{1,0:T(8,128)(2,1)} %param.8) | non-fusion elementwise | flops 2359296 | bytes 14155776 | tf_op jit(solution)/shard_map/convert_element_type | solution.py:35
  153.0 0.6 dynamic-slice
  154.3 0.1 convert_reduce_fusion.1
  154.4 0.2 fusion.17
  154.6 0.6 multiply_reduce_fusion.2
  155.3 30.6 %all_gather.15 = bf16[64,1152]{1,0:T(8,128)(2,1)S(1)} all-gather(bf16[8,1152]{1,0:T(8,128)(2,1)S(1)} %divide_convert_fusion), channel_id=1, replica_groups=mesh['dp'=8,'mp'=4] {'dp'}, dimensions={0}, use_global_device_ids=true | all-gather | bytes 165888 | tf_op jit(solution)/shard_map/all_gather | solution.py:66
  185.9 4.5 %reduce-scatter.2.cloned.1.call-done = bf16[512,1152]{1,0:T(8,128)(2,1)} async-done(((bf16[2048,1152]{1,0:T(8,128)(2,1)}), bf16[512,1152]{1,0:T(8,128)(2,1)}) %reduce-scatter.2.cloned.1.call-update) | async-done | bytes 1179664 | tf_op jit(solution)/shard_map/reduce_scatter | solution.py:46
  190.4 2.4 %fusion.14 = f32[512]{0:T(512)S(1)} fusion(bf16[512,1152]{1,0:T(8,128)(2,1)} %reduce-scatter.2.cloned.1.call-done, f32[2048,1152]{1,0:T(8,128)} %convert_element_type.27, s32[]{:T(128)S(6)} %select_n.12), kind=kLoop, calls=%fused_computation.24 | loop fusion | flops 1768960 | bytes 3540996 | tf_op jit(solution)/shard_map/reduce_sum | solution.py:10
  192.9 2.5 %multiply_reduce_fusion.1 = f32[512]{0:T(512)S(1)} fusion(f32[512]{0:T(512)S(1)} %broadcast_multiply_fusion.1, bf16[512,1152]{1,0:T(8,128)(2,1)} %reduce-scatter.2.cloned.1.call-done, f32[2048,1152]{1,0:T(8,128)} %convert_element_type.27, s32[]{:T(128)S(6)} %select_n.12), kind=kLoop, calls=%fused_computation.19 | loop fusion | flops 2948608 | bytes 3543044 | tf_op jit(solution)/shard_map/reduce_sum | solution.py:12
  195.4 2.2 bitcast_reduce_fusion
  197.6 0.1 multiply_reduce_fusion.3
  197.7 0.1 fusion.25
  197.8 5.2 %all-gather = bf16[4,2,1152]{2,1,0:T(2,128)(2,1)S(1)} all-gather(bf16[1,2,1152]{2,1,0:T(2,128)(2,1)S(1)} %fusion.25), channel_id=1, replica_groups=mesh['dp'=8,'mp'=4] {'mp'}, dimensions={0}, use_global_device_ids=true | all-gather | bytes 23040 | tf_op jit(solution)/shard_map/all_gather | solution.py:54
  203.0 0.8 fusion.30
  203.8 21.3 %all-reduce = f32[64]{0:T(128)S(1)} all-reduce(f32[64]{0:T(128)S(1)} %get-tuple-element.5), channel_id=3, replica_groups=mesh['dp'=8,'mp'=4] {'dp'}, use_global_device_ids=true, to_apply=%region_12.13.clone | all-reduce | flops 64 | bytes 512
  225.2 0.6 dynamic-slice.1
  (25 shorter events, 0.3 us)
Async XLA Ops:
  7.2 147.4 %copy-start = (bf16[1152,1152]{1,0:T(8,128)(2,1)S(1)}, bf16[1152,1152]{1,0:T(8,128)(2,1)}, u32[]{:S(2)}) copy-start(bf16[1152,1152]{1,0:T(8,128)(2,1)} %param.13) | copy-start | bytes 7962628
  7.2 60.7 %all-gather.4.cloned.1.call-start = ((), (), s32[]{:S(2)}) async-start(), calls=%async_computation.1 | async-start | bytes 2985984 | tf_op jit(solution)/shard_map/all_gather | solution.py:37
  7.9 115.7 %all-gather.6.cloned.1.call-start = ((), (), s32[]{:S(2)}) async-start(), calls=%async_computation.2 | async-start | bytes 2985984 | tf_op jit(solution)/shard_map/all_gather | solution.py:43
  8.7 181.8 %reduce-scatter.2.cloned.1.call-start = ((), (), s32[]{:S(2)}) async-start(), calls=%async_computation.3 | async-start | bytes 5898240 | tf_op jit(solution)/shard_map/reduce_scatter | solution.py:46
  8.7 4.2 %copy-start.1 = (bf16[2048,1152]{1,0:T(8,128)(2,1)S(1)}, bf16[2048,1152]{1,0:T(8,128)(2,1)}, u32[]{:S(2)}) copy-start(bf16[2048,1152]{1,0:T(8,128)(2,1)} %param.8) | copy-start | bytes 14155780
  143.7 9.3 %copy-start.4 = (u32[32]{0:T(128)S(1)}, u32[32]{0:T(128)}, u32[]{:S(2)}) copy-start(u32[32]{0:T(128)} %constant.53) | copy-start | bytes 388
  143.7 10.5 %copy-start.3 = (bf16[8,1152]{1,0:T(8,128)(2,1)S(1)}, bf16[8,1152]{1,0:T(8,128)(2,1)}, u32[]{:S(2)}) copy-start(bf16[8,1152]{1,0:T(8,128)(2,1)} %param.9) | copy-start | bytes 55300
  190.4 5.0 %copy-start.2 = (bf16[512,1152]{1,0:T(8,128)(2,1)S(1)}, bf16[512,1152]{1,0:T(8,128)(2,1)}, u32[]{:S(2)}) copy-start(bf16[512,1152]{1,0:T(8,128)(2,1)} %reduce-scatter.2.cloned.1.call-done) | copy-start | bytes 3538948
Sparse Core Ops, SparseCore 0:
  10.2 57.6 all-gather.3
  70.1 53.5 all-gather.5
  143.8 46.5 reduce-scatter.1
where the time goes:
time: 233 us; the launch traced here: 232 us
  waiting for transfers between devices  115 us (49%)
  blocking collectives  57.1 us (25%)
  matrix products  21.5 us (9%)
  other arithmetic  20.3 us (9%)
  between operations  15.8 us (7%)
    all_gather x1, waiting for transfers between devices, on_device(): lax.all_gather(contracting_matrix, 'dp', axis=1, tiled=True)  55.8 us
    all_gather x1, waiting for transfers between devices, on_device(): inner_weight = lax.all_gather(widening_matrix, 'dp', axis=0, tiled=True)  53.6 us
    all_gather x1, blocking collectives, on_device(): lax.all_gather(caption_code_direction, 'dp', axis=0, tiled=True)  30.6 us
    unnamed x1, blocking collectives  21.3 us
    dot_general x1, matrix products, on_device(): jnp.dot(image_units, lax.all_gather(contracting_matrix, 'dp', axis=1, til...  20 us
    convert_element_type x1, other arithmetic, on_device(): image_rows = picture_skip_activations.astype(jnp.float32)  7.92 us
    reduce_sum x3, other arithmetic, layer_norm(): average = jnp.mean(values, axis=-1, keepdims=True)  5.79 us
    all_gather x1, blocking collectives, on_device(): picture_code_direction = lax.all_gather(own_emb, 'mp', axis=0, tiled=True)  5.21 us
  transfers between devices with their start and end apart: 3, of which 3 were waited for; matrix products, arithmetic and copies ran while one was open for 7% of the time, Pallas kernels for 0%

commit v1 on v0

--- a/solution.py
+++ b/solution.py
@@ -1,6 +1,10 @@
+import functools
+
 import jax
 import jax.numpy as jnp
 from jax import lax
+from jax.experimental import pallas as pl
+from jax.experimental.pallas import tpu as pltpu
 from jax.sharding import PartitionSpec as P
 
 PATCHES = 256
@@ -77,9 +81,470 @@
     return (row_loss, col_loss)
 
 
+MESH = pl.DeviceIdType.MESH
+ROW_TILE = 256
+LANES = 128
+
+
+def dot_nt(a, b):
+    return lax.dot_general(a, b, (((1,), (1,)), ((), ())), preferred_element_type=jnp.float32)
+
+
+def fused_kernel(
+    n_dp,
+    n_mp,
+    x_hbm,
+    text_ref,
+    gain_ref,
+    w1_own,
+    w2_own,
+    map_hbm,
+    sharp_ref,
+    offset_ref,
+    out_ref,
+    x_buf,
+    xn_buf,
+    map_buf,
+    w1_full,
+    w2_full,
+    units,
+    partial,
+    core_in,
+    cross_out,
+    cross_in,
+    final,
+    texts,
+    message,
+    slots,
+    local_sem,
+    y_send,
+    z_send,
+    w_recv,
+    text_send,
+    text_recv,
+    core_send,
+    core_recv,
+    cross_send,
+    cross_recv,
+    msg_send,
+    msg_recv,
+):
+    dp = lax.axis_index("dp")
+    mp = lax.axis_index("mp")
+    n_all = n_dp * n_mp
+    me = dp * n_mp + mp
+    rows, width = x_buf.shape
+    block = w1_own.shape[0]
+    own_rows = rows // n_mp
+    own_images = own_rows // PATCHES
+    dev_images = rows // PATCHES
+    dev_texts = text_ref.shape[0]
+    pairs = n_dp * dev_texts
+    tiles = rows // ROW_TILE
+    nz = n_dp // 2
+    z, y = lax.div(dp, 2), lax.rem(dp, 2)
+    y_peer = dp + 1 - 2 * y
+    core = lax.rem(mp, 2)
+    sibling = mp + 1 - 2 * core
+    across = lax.rem(mp + 2, n_mp)
+    pair = 2 * block
+
+    shorter = jnp.minimum(z, nz - 1 - z)
+    toward = jnp.where(z < nz - 1 - z, 1, -1)
+    order, sides = [z], [None]
+    for j in range(1, nz):
+        sign = jnp.where(j <= 2 * shorter, 1 if j % 2 else -1, toward)
+        hop = jnp.where(j <= 2 * shorter, (j + 1) // 2, j - shorter)
+        order.append(z + sign * hop)
+        sides.append(sign)
+
+    x_copy = pltpu.make_async_copy(x_hbm, x_buf, local_sem.at[0])
+    map_copy = pltpu.make_async_copy(map_hbm, map_buf, local_sem.at[1])
+    x_copy.start()
+    map_copy.start()
+
+    barrier = pltpu.get_barrier_semaphore()
+
+    def greet(k, carry):
+        peer = lax.rem(me + k, n_all)
+        pl.semaphore_signal(
+            barrier, inc=1, device_id=(lax.div(peer, n_mp), lax.rem(peer, n_mp)), device_id_type=MESH
+        )
+        return carry
+
+    lax.fori_loop(1, n_all, greet, 0)
+
+    full = (w1_full, w2_full)
+    own = (w1_own, w2_own)
+
+    def span(d):
+        return pl.ds(pl.multiple_of(d * block, block), block)
+
+    def weight_copy(w, d, is_own, target, send_sem):
+        return pltpu.make_async_remote_copy(
+            src_ref=own[w] if is_own else full[w].at[span(d)],
+            dst_ref=full[w].at[span(d)],
+            send_sem=send_sem,
+            recv_sem=w_recv.at[w, d],
+            device_id=(target, mp),
+            device_id_type=MESH,
+        )
+
+    def y_copy(w, j):
+        return weight_copy(w, 2 * order[j] + y, j == 0, y_peer, y_send.at[w, j])
+
+    def own_z_copy(w, sign):
+        return weight_copy(w, dp, True, dp + 2 * sign, z_send.at[w, 0 if sign > 0 else nz])
+
+    def pass_on_copy(w, j):
+        return weight_copy(w, 2 * order[j] + y, False, dp - 2 * sides[j], z_send.at[w, j])
+
+    def can_pass(j):
+        there = z - sides[j]
+        return jnp.logical_and(there >= 0, there < nz)
+
+    def start_own(w):
+        @pl.when(z + 1 < nz)
+        def _():
+            own_z_copy(w, 1).start()
+
+        @pl.when(z >= 1)
+        def _():
+            own_z_copy(w, -1).start()
+
+        y_copy(w, 0).start()
+
+    def wait_block(w, d):
+        pltpu.make_async_copy(own[w], full[w].at[span(d)], w_recv.at[w, d]).wait()
+
+    def pass_on(w, j):
+        wait_block(w, 2 * order[j] + y)
+
+        @pl.when(can_pass(j))
+        def _():
+            pass_on_copy(w, j).start()
+
+        y_copy(w, j).start()
+
+    pl.semaphore_wait(barrier, n_all - 1)
+    start_own(0)
+
+    w1_full[span(dp), :] = w1_own[...]
+    w2_full[span(dp), :] = w2_own[...]
+
+    map_copy.wait()
+    text_normed = layer_norm(text_ref[...].astype(jnp.float32), gain_ref[2:3, :]).astype(jnp.bfloat16)
+    text_vector = jnp.dot(text_normed, map_buf[...], preferred_element_type=jnp.float32)
+    texts[dp] = unit_vector(text_vector)
+
+    def text_copy(k):
+        return pltpu.make_async_remote_copy(
+            src_ref=texts.at[dp],
+            dst_ref=texts.at[dp],
+            send_sem=text_send.at[k],
+            recv_sem=text_recv.at[k],
+            device_id=(lax.rem(dp + k, n_dp), mp),
+            device_id_type=MESH,
+        )
+
+    for k in range(1, n_dp):
+        text_copy(k).start()
+
+    x_copy.wait()
+
+    def normalise(t, carry):
+        r = pl.ds(pl.multiple_of(t * ROW_TILE, ROW_TILE), ROW_TILE)
+        xn_buf[r, :] = layer_norm(x_buf[r, :].astype(jnp.float32), gain_ref[0:1, :]).astype(jnp.bfloat16)
+        return carry
+
+    lax.fori_loop(0, tiles // 2, normalise, 0)
+    pass_on(0, 1)
+    lax.fori_loop(tiles // 2, tiles, normalise, 0)
+    for j in range(2, nz):
+        pass_on(0, j)
+    start_own(1)
+
+    for t in range(own_rows // ROW_TILE):
+        r = pl.ds(pl.multiple_of(mp * own_rows + t * ROW_TILE, ROW_TILE), ROW_TILE)
+        final[:, t * ROW_TILE : (t + 1) * ROW_TILE] = x_buf[r, :].astype(jnp.float32).T
+
+    for j in range(nz):
+        wait_block(0, 2 * order[j] + 1 - y)
+
+    def widen(t, carry):
+        r = pl.ds(pl.multiple_of(t * ROW_TILE, ROW_TILE), ROW_TILE)
+        hidden = jnp.dot(xn_buf[r, :], w1_full[...], preferred_element_type=jnp.float32)
+        units[r, :] = jax.nn.gelu(hidden, approximate=True).astype(jnp.bfloat16)
+        return carry
+
+    lax.fori_loop(0, tiles // 2, widen, 0)
+    pass_on(1, 1)
+    lax.fori_loop(tiles // 2, tiles, widen, 0)
+
+    def group(j):
+        return pl.ds(pl.multiple_of(order[j] * pair, pair), pair)
+
+    def quarter(q):
+        return pl.ds(pl.multiple_of(q * own_rows, own_rows), own_rows)
+
+    sides_x = n_mp // 2
+    my_side = lax.div(mp, 2)
+
+    def core_copy(j, s):
+        return pltpu.make_async_remote_copy(
+            src_ref=partial.at[group(j), quarter(2 * s + 1 - core)],
+            dst_ref=core_in.at[group(j), pl.ds(s * own_rows, own_rows)],
+            send_sem=core_send.at[j, s],
+            recv_sem=core_recv.at[j, s],
+            device_id=(dp, sibling),
+            device_id_type=MESH,
+        )
+
+    def cross_copy(j):
+        return pltpu.make_async_remote_copy(
+            src_ref=cross_out.at[group(j)],
+            dst_ref=cross_in.at[group(j)],
+            send_sem=cross_send.at[j],
+            recv_sem=cross_recv.at[j],
+            device_id=(dp, across),
+            device_id_type=MESH,
+        )
+
+    def contract(j):
+        wait_block(1, 2 * order[j] + 1 - y)
+        weight = w2_full[group(j), :]
+        for t in range(n_mp):
+            r = pl.ds(t * own_rows, own_rows)
+            partial[group(j), r] = dot_nt(weight, units[r, :]).astype(jnp.bfloat16)
+        for s in range(sides_x):
+            core_copy(j, s).start()
+
+    def meet(j):
+        for s in range(sides_x):
+            core_copy(j, s).wait_recv()
+        g = group(j)
+        there = lax.rem(my_side + 1, sides_x)
+        summed = partial[g, quarter(across)].astype(jnp.float32) + core_in[g, quarter(there)].astype(jnp.float32)
+        cross_out[g, :] = summed.astype(jnp.bfloat16)
+        cross_copy(j).start()
+        final[g, :] = (
+            final[g, :]
+            + partial[g, quarter(mp)].astype(jnp.float32)
+            + core_in[g, quarter(my_side)].astype(jnp.float32)
+        )
+
+    for j in range(nz):
+        if j + 1 < nz and j >= 1:
+            pass_on(1, j + 1)
+        contract(j)
+        if j == 0 and nz > 2:
+            pass
+        if j >= 1:
+            meet(j - 1)
+    meet(nz - 1)
+
+    for j in range(nz):
+        cross_copy(j).wait_recv()
+        final[group(j), :] = final[group(j), :] + cross_in[group(j), :].astype(jnp.float32)
+
+    value = final[...]
+    average = jnp.mean(value, axis=0, keepdims=True)
+    centred = value - average
+    spread = jnp.mean(centred * centred, axis=0, keepdims=True)
+    scaled = centred * lax.rsqrt(spread + 1e-06)
+    pooled = jnp.zeros((8, width), jnp.float32)
+    row_place = lax.broadcasted_iota(jnp.int32, (8, width), 0)
+    for image in range(own_images):
+        folded = jnp.zeros((width, LANES), jnp.float32)
+        for c in range(PATCHES // LANES):
+            first = image * PATCHES + c * LANES
+            folded = folded + scaled[:, first : first + LANES]
+        one = jnp.sum(folded.T, axis=0, keepdims=True) * (1.0 / PATCHES)
+        pooled = jnp.where(row_place == image, one, pooled)
+    image_emb = unit_vector(pooled * gain_ref[1:2, :])
+
+    for k in range(1, n_dp):
+        text_copy(k).wait_recv()
+    every_text = texts[...].astype(jnp.float32).reshape(pairs, width)
+    every_text = jnp.concatenate([every_text, jnp.zeros((LANES - pairs, width), jnp.float32)], axis=0)
+    scores = sharp_ref[0] * dot_nt(image_emb, every_text.astype(jnp.bfloat16)) + offset_ref[0]
+    row = lax.broadcasted_iota(jnp.int32, scores.shape, 0)
+    col = lax.broadcasted_iota(jnp.int32, scores.shape, 1)
+    own_row = row < own_images
+    matching = row + dp * dev_images + mp * own_images == col
+    signed = jnp.where(matching, -scores, scores)
+    terms = jnp.maximum(signed, 0.0) + jnp.log1p(jnp.exp(-jnp.abs(signed)))
+    terms = jnp.where(jnp.logical_and(own_row, col < pairs), terms, 0.0)
+    row_sum = jnp.sum(terms, axis=1, keepdims=True)
+    terms = terms + jnp.where(jnp.logical_and(own_row, col == pairs + row), row_sum, 0.0)
+    sent = jnp.sum(terms, axis=0, keepdims=True)
+    message[...] = sent
+    slots[me] = sent
+
+    def msg_copy(k):
+        peer = lax.rem(me + k, n_all)
+        return pltpu.make_async_remote_copy(
+            src_ref=message,
+            dst_ref=slots.at[me],
+            send_sem=msg_send.at[k],
+            recv_sem=msg_recv.at[k],
+            device_id=(lax.div(peer, n_mp), lax.rem(peer, n_mp)),
+            device_id_type=MESH,
+        )
+
+    def send_msg(k, carry):
+        msg_copy(k).start()
+        return carry
+
+    lax.fori_loop(1, n_all, send_msg, 0)
+
+    for w in range(2):
+        @pl.when(z + 1 < nz)
+        def _():
+            own_z_copy(w, 1).wait_send()
+
+        @pl.when(z >= 1)
+        def _():
+            own_z_copy(w, -1).wait_send()
+
+        for j in range(nz):
+            y_copy(w, j).wait_send()
+            if j >= 1:
+
+                @pl.when(can_pass(j))
+                def _():
+                    pass_on_copy(w, j).wait_send()
+
+    for k in range(1, n_dp):
+        text_copy(k).wait_send()
+    for j in range(nz):
+        for s in range(sides_x):
+            core_copy(j, s).wait_send()
+        cross_copy(j).wait_send()
+
+    def end_msg(k, carry):
+        msg_copy(k).wait()
+        return carry
+
+    lax.fori_loop(1, n_all, end_msg, 0)
+
+    total = jnp.zeros((1, LANES), jnp.float32)
+    for s in range(n_all):
+        total = total + slots[s]
+    lane = lax.broadcasted_iota(jnp.int32, (1, LANES), 1)
+    place = lax.broadcasted_iota(jnp.int32, (dev_texts, LANES), 0)
+    wide = lax.broadcasted_iota(jnp.int32, (dev_texts, LANES), 1)
+    picked = jnp.where(wide == dp * dev_texts + place, jnp.broadcast_to(total, wide.shape), 0.0)
+    col_own = jnp.sum(picked, axis=1, keepdims=True)
+    place_r = lax.broadcasted_iota(jnp.int32, (dev_images, LANES), 0)
+    wide_r = lax.broadcasted_iota(jnp.int32, (dev_images, LANES), 1)
+    row_own = jnp.zeros((dev_images, 1), jnp.float32)
+    for m in range(n_mp):
+        theirs = jnp.broadcast_to(slots[dp * n_mp + m], wide_r.shape)
+        mine = jnp.logical_and(
+            wide_r - pairs == place_r - m * own_images,
+            jnp.logical_and(wide_r >= pairs, wide_r < pairs + own_images),
+        )
+        row_own = row_own + jnp.sum(jnp.where(mine, theirs, 0.0), axis=1, keepdims=True)
+    out_ref[...] = jnp.where(wide == 0, row_own, col_own)
+
+
+def fused(
+    n_dp,
+    n_mp,
+    picture_skip_activations,
+    caption_closing_activations,
+    normaliser_multipliers,
+    widening_matrix,
+    contracting_matrix,
+    caption_mapping_matrix,
+    sharpness_factor,
+    score_offset_term,
+):
+    rows, width = picture_skip_activations.shape
+    block, hidden = widening_matrix.shape
+    extra = -hidden % LANES
+    hidden += extra
+    w1 = jnp.pad(widening_matrix, ((0, 0), (0, extra)))
+    w2 = jnp.pad(contracting_matrix, ((0, extra), (0, 0))).T
+    own_rows = rows // n_mp
+    nz, sides_x, n_all = n_dp // 2, n_mp // 2, n_dp * n_mp
+    dev_texts = caption_closing_activations.shape[0]
+    bf16, f32 = jnp.bfloat16, jnp.float32
+    vmem = pl.BlockSpec(memory_space=pltpu.VMEM)
+    hbm = pl.BlockSpec(memory_space=pl.ANY)
+    smem = pl.BlockSpec(memory_space=pltpu.SMEM)
+    dma = pltpu.SemaphoreType.DMA
+    out = pl.pallas_call(
+        functools.partial(fused_kernel, n_dp, n_mp),
+        out_shape=jax.ShapeDtypeStruct((dev_texts, LANES), f32),
+        in_specs=[hbm, vmem, vmem, vmem, vmem, hbm, smem, smem],
+        out_specs=vmem,
+        scratch_shapes=[
+            pltpu.VMEM((rows, width), bf16),
+            pltpu.VMEM((rows, width), bf16),
+            pltpu.VMEM((width, width), bf16),
+            pltpu.VMEM((width, hidden), bf16),
+            pltpu.VMEM((width, hidden), bf16),
+            pltpu.VMEM((rows, hidden), bf16),
+            pltpu.VMEM((width, rows), bf16),
+            pltpu.VMEM((width, sides_x * own_rows), bf16),
+            pltpu.VMEM((width, own_rows), bf16),
+            pltpu.VMEM((width, own_rows), bf16),
+            pltpu.VMEM((width, own_rows), f32),
+            pltpu.VMEM((n_dp, dev_texts, width), bf16),
+            pltpu.VMEM((1, LANES), f32),
+            pltpu.VMEM((n_all, 1, LANES), f32),
+            dma((2,)),
+            dma((2, nz)),
+            dma((2, nz + 1)),
+            dma((2, n_dp)),
+            dma((n_dp,)),
+            dma((n_dp,)),
+            dma((nz, sides_x)),
+            dma((nz, sides_x)),
+            dma((nz,)),
+            dma((nz,)),
+            dma((n_all,)),
+            dma((n_all,)),
+        ],
+        compiler_params=pltpu.CompilerParams(
+            collective_id=0, has_side_effects=True, vmem_limit_bytes=60 * 1024 * 1024
+        ),
+    )(
+        picture_skip_activations,
+        caption_closing_activations,
+        normaliser_multipliers,
+        w1,
+        w2,
+        caption_mapping_matrix,
+        sharpness_factor,
+        score_offset_term,
+    )
+    return out[:, 0], out[:, 1]
+
+
+def pick(n_dp, n_mp, *args):
+    pictures, captions, _, widening = args[:4]
+    rows, width = pictures.shape
+    pairs = captions.shape[0] * n_dp
+    fits = (
+        n_dp % 2 == 0
+        and n_dp >= 4
+        and n_mp == 4
+        and widening.shape[0] % 16 == 0
+        and rows % (n_mp * PATCHES) == 0
+        and width % LANES == 0
+        and rows // PATCHES == captions.shape[0]
+        and captions.shape[0] % 8 == 0
+        and pairs + rows // (n_mp * PATCHES) <= LANES
+    )
+    return fused(n_dp, n_mp, *args) if fits else on_device(*args)
+
+
 def solution(mesh):
     return jax.shard_map(
-        on_device,
+        functools.partial(pick, mesh.shape["dp"], mesh.shape["mp"]),
         mesh=mesh,
         in_specs=(P("dp", None), P("dp", None), P(), P("dp", "mp"), P("mp", "dp"), P(), P(), P()),
         out_specs=(P("dp"), P("dp")),

time: 233 us -> 101 us (0.43)
  waiting for transfers between devices: 115 us -> 0 us
  Pallas kernels: 0 us -> 93.9 us
  blocking collectives: 57.1 us -> 0 us
  matrix products: 21.5 us -> 0 us
  other arithmetic: 20.3 us -> 0 us
  between operations: 15.8 us -> 1.93 us
  local copies, waits for them, and re-layouts: 2.17 us -> 4.92 us
    all_gather x2 -> x0, waiting for transfers between devices: 109 us -> none  [the longest x1 55.8 us: on_device(): lax.all_gather(contracting_matrix, 'dp', axis=1, tiled=True)]
    pallas_call x0 -> x1, Pallas kernels: none -> 93.9 us  [fused(): pl.pallas_call(functools.partial(fused_kernel, n_dp, n_mp), out_shape=jax...]
    all_gather x2 -> x0, blocking collectives: 35.8 us -> none  [the longest x1 30.6 us: on_device(): lax.all_gather(caption_code_direction, 'dp', axis=0, tiled=True)]
    dot_general x3 -> x0, matrix products: 21.5 us -> none  [the longest x1 20 us: on_device(): jnp.dot(image_units, lax.all_gather(contracting_matrix, 'dp', axis=1, til...]
    unnamed x1 -> x0, blocking collectives: 21.3 us -> none
    reduce_sum x8 -> x0, other arithmetic: 12.2 us -> none  [the longest x3 5.79 us: layer_norm(): average = jnp.mean(values, axis=-1, keepdims=True)]
    convert_element_type x2 -> x0, other arithmetic: 7.99 us -> none  [the longest x1 7.92 us: on_device(): image_rows = picture_skip_activations.astype(jnp.float32)]
    reduce_scatter x1 -> x0, waiting for transfers between devices: 4.55 us -> none  [on_device(): lax.psum_scatter(partial_out.astype(jnp.bfloat16), 'mp', scatter_dimensio...]
  transfers between devices with their start and end apart: 3 -> 0, of which waited for: 3 -> 0; matrix products, arithmetic and copies ran while one was open for 7% -> 0% of each run, Pallas kernels for 0% -> 0%
where the time goes in v1:
time: 101 us
  Pallas kernels  93.9 us (93%)
  local copies, waits for them, and re-layouts  4.92 us (5%)
  between operations  1.93 us (2%)
    pallas_call x1, Pallas kernels, fused(): pl.pallas_call(functools.partial(fused_kernel, n_dp, n_mp), out_shape=jax...  93.9 us

profile of v1, /device:TPU:0, one launch (start us, length us, event | category | flops | bytes accessed | tf_op | source)
XLA Modules:
  0.0 100.8 jit_solution(2920752661508546676)
XLA Ops:
  1.9 1.7 %pad.8.w1_own = bf16[144,1152]{1,0:T(8,128)(2,1)} pad(bf16[144,1076]{1,0:T(8,128)(2,1)} %param.11, bf16[]{:T(256)} %constant.2.clone.1), padding=0_0x0_76 | pad | bytes 641666 | tf_op jit(solution)/shard_map/jit(_pad)/pad | solution.py:468
  3.6 1.7 %pad_bitcast_fusion.w2_own = bf16[144,1152]{1,0:T(8,128)(2,1)} fusion(bf16[1076,144]{0,1:T(8,128)(2,1)} %param.12), kind=kLoop, calls=%fused_computation | loop fusion | bytes 641664 | tf_op jit(solution)/shard_map/transpose | solution.py:469
  5.4 93.9 %shard_map.95 = f32[8,128]{1,0:T(8,128)} custom-call(bf16[2048,1152]{1,0:T(8,128)(2,1)} %x_hbm.1, bf16[8,1152]{1,0:T(8,128)(2,1)} %text_ref.1, f32[3,1152]{1,0:T(4,128)} %gain_ref.1, bf16[144,1152]{1,0:T(8,128)(2,1)} %pad.8.w1_own, bf16[144,1152]{1,0:T(8,128)(2,1)} %pad_bitcast_fusion.w2_own, bf16[1152,1152]{1,0:T(8,128)(2,1)} %map_hbm.1, ...), custom_call_target="tpu_custom_call" | custom-call | tf_op jit(solution)/shard_map/pallas_call | solution.py:478
  99.3 1.5 %slice_reduce_fusion = (f32[8]{0:T(128)}, f32[8]{0:T(128)}) fusion(f32[8,128]{1,0:T(8,128)} %shard_map.95), kind=kLoop, calls=%fused_computation.1 | loop fusion | bytes 128 | tf_op jit(solution)/shard_map/slice | solution.py:524

commit v2 on v1

--- a/solution.py
+++ b/solution.py
@@ -120,8 +120,6 @@
     y_send,
     z_send,
     w_recv,
-    text_send,
-    text_recv,
     core_send,
     core_recv,
     cross_send,
@@ -174,102 +172,144 @@
 
     lax.fori_loop(1, n_all, greet, 0)
 
-    full = (w1_full, w2_full)
-    own = (w1_own, w2_own)
-
-    def span(d):
-        return pl.ds(pl.multiple_of(d * block, block), block)
-
-    def weight_copy(w, d, is_own, target, send_sem):
+    pieces = next(c for c in (3, 2, 1) if block % (16 * c) == 0)
+    piece = block // pieces
+    counts = (pieces, pieces, 1)
+
+    def own_part(w, c):
+        if w == 2:
+            return texts.at[dp]
+        return (w1_own, w2_own)[w].at[pl.ds(c * piece, piece)]
+
+    def part(w, d, c):
+        if w == 2:
+            return texts.at[d]
+        return (w1_full, w2_full)[w].at[pl.ds(pl.multiple_of(d * block + c * piece, 16), piece)]
+
+    def gather_copy(w, d, c, is_own, target, send_sem):
         return pltpu.make_async_remote_copy(
-            src_ref=own[w] if is_own else full[w].at[span(d)],
-            dst_ref=full[w].at[span(d)],
+            src_ref=own_part(w, c) if is_own else part(w, d, c),
+            dst_ref=part(w, d, c),
             send_sem=send_sem,
-            recv_sem=w_recv.at[w, d],
+            recv_sem=w_recv.at[w, d, c],
             device_id=(target, mp),
             device_id_type=MESH,
         )
 
-    def y_copy(w, j):
-        return weight_copy(w, 2 * order[j] + y, j == 0, y_peer, y_send.at[w, j])
-
-    def own_z_copy(w, sign):
-        return weight_copy(w, dp, True, dp + 2 * sign, z_send.at[w, 0 if sign > 0 else nz])
-
-    def pass_on_copy(w, j):
-        return weight_copy(w, 2 * order[j] + y, False, dp - 2 * sides[j], z_send.at[w, j])
+    def y_copy(w, j, c):
+        return gather_copy(w, 2 * order[j] + y, c, j == 0, y_peer, y_send.at[w, j, c])
+
+    def own_z_copy(w, sign, c):
+        return gather_copy(w, dp, c, True, dp + 2 * sign, z_send.at[w, 0 if sign > 0 else nz, c])
+
+    def pass_on_copy(w, j, c):
+        return gather_copy(w, 2 * order[j] + y, c, False, dp - 2 * sides[j], z_send.at[w, j, c])
 
     def can_pass(j):
         there = z - sides[j]
         return jnp.logical_and(there >= 0, there < nz)
 
+    def start_z(w, sign):
+        for c in range(counts[w]):
+            own_z_copy(w, sign, c).start()
+
+    def start_y(w, j):
+        for c in range(counts[w]):
+            y_copy(w, j, c).start()
+
     def start_own(w):
         @pl.when(z + 1 < nz)
         def _():
-            own_z_copy(w, 1).start()
+            start_z(w, 1)
 
         @pl.when(z >= 1)
         def _():
-            own_z_copy(w, -1).start()
-
-        y_copy(w, 0).start()
+            start_z(w, -1)
+
+        start_y(w, 0)
+
+    def wait_part(w, d, c):
+        pltpu.make_async_copy(own_part(w, c), part(w, d, c), w_recv.at[w, d, c]).wait()
 
     def wait_block(w, d):
-        pltpu.make_async_copy(own[w], full[w].at[span(d)], w_recv.at[w, d]).wait()
+        for c in range(counts[w]):
+            wait_part(w, d, c)
 
     def pass_on(w, j):
-        wait_block(w, 2 * order[j] + y)
-
-        @pl.when(can_pass(j))
-        def _():
-            pass_on_copy(w, j).start()
-
-        y_copy(w, j).start()
-
-    pl.semaphore_wait(barrier, n_all - 1)
+        for c in range(counts[w]):
+            wait_part(w, 2 * order[j] + y, c)
+
+            @pl.when(can_pass(j))
+            def _():
+                pass_on_copy(w, j, c).start()
+
+            y_copy(w, j, c).start()
+
+    with jax.named_scope("barrier"):
+        pl.semaphore_wait(barrier, n_all - 1)
     start_own(0)
 
-    w1_full[span(dp), :] = w1_own[...]
-    w2_full[span(dp), :] = w2_own[...]
-
-    map_copy.wait()
+    w1_full[pl.ds(pl.multiple_of(dp * block, block), block), :] = w1_own[...]
+    w2_full[pl.ds(pl.multiple_of(dp * block, block), block), :] = w2_own[...]
+
+    with jax.named_scope("mapwait"):
+        map_copy.wait()
     text_normed = layer_norm(text_ref[...].astype(jnp.float32), gain_ref[2:3, :]).astype(jnp.bfloat16)
     text_vector = jnp.dot(text_normed, map_buf[...], preferred_element_type=jnp.float32)
     texts[dp] = unit_vector(text_vector)
 
-    def text_copy(k):
-        return pltpu.make_async_remote_copy(
-            src_ref=texts.at[dp],
-            dst_ref=texts.at[dp],
-            send_sem=text_send.at[k],
-            recv_sem=text_recv.at[k],
-            device_id=(lax.rem(dp + k, n_dp), mp),
-            device_id_type=MESH,
-        )
-
-    for k in range(1, n_dp):
-        text_copy(k).start()
-
-    x_copy.wait()
+    start_own(2)
+
+    @pl.when(z == 0)
+    def _():
+        start_z(1, 1)
+
+    @pl.when(z == nz - 1)
+    def _():
+        start_z(1, -1)
+
+    with jax.named_scope("xwait"):
+        x_copy.wait()
 
     def normalise(t, carry):
         r = pl.ds(pl.multiple_of(t * ROW_TILE, ROW_TILE), ROW_TILE)
         xn_buf[r, :] = layer_norm(x_buf[r, :].astype(jnp.float32), gain_ref[0:1, :]).astype(jnp.bfloat16)
         return carry
 
-    lax.fori_loop(0, tiles // 2, normalise, 0)
-    pass_on(0, 1)
-    lax.fori_loop(tiles // 2, tiles, normalise, 0)
+    with jax.named_scope("ln0"):
+        lax.fori_loop(0, tiles // 2, normalise, 0)
+    def pass_first(j):
+        with jax.named_scope(f"pass_w1_{j}"):
+            pass_on(0, j)
+        with jax.named_scope(f"pass_text_{j}"):
+            pass_on(2, j)
+
+        @pl.when(jnp.logical_and(order[j] == 0, z + 1 < nz))
+        def _():
+            start_z(1, 1)
+
+        @pl.when(jnp.logical_and(order[j] == nz - 1, z >= 1))
+        def _():
+            start_z(1, -1)
+
+    pass_first(1)
+    with jax.named_scope("ln1"):
+        lax.fori_loop(tiles // 2, tiles, normalise, 0)
     for j in range(2, nz):
-        pass_on(0, j)
-    start_own(1)
+        pass_first(j)
+    start_y(1, 0)
 
     for t in range(own_rows // ROW_TILE):
         r = pl.ds(pl.multiple_of(mp * own_rows + t * ROW_TILE, ROW_TILE), ROW_TILE)
         final[:, t * ROW_TILE : (t + 1) * ROW_TILE] = x_buf[r, :].astype(jnp.float32).T
 
-    for j in range(nz):
-        wait_block(0, 2 * order[j] + 1 - y)
+    for j in range(nz - 1):
+        with jax.named_scope(f"wait_w1y_{j}"):
+            wait_block(0, 2 * order[j] + 1 - y)
+    with jax.named_scope("pass_w2_1"):
+        pass_on(1, 1)
+    with jax.named_scope("wait_w1y_last"):
+        wait_block(0, 2 * order[nz - 1] + 1 - y)
 
     def widen(t, carry):
         r = pl.ds(pl.multiple_of(t * ROW_TILE, ROW_TILE), ROW_TILE)
@@ -277,12 +317,19 @@
         units[r, :] = jax.nn.gelu(hidden, approximate=True).astype(jnp.bfloat16)
         return carry
 
-    lax.fori_loop(0, tiles // 2, widen, 0)
-    pass_on(1, 1)
-    lax.fori_loop(tiles // 2, tiles, widen, 0)
+    with jax.named_scope("widen0"):
+        lax.fori_loop(0, tiles // 2, widen, 0)
+    if nz > 2:
+        with jax.named_scope("pass_w2_2"):
+            pass_on(1, 2)
+    with jax.named_scope("widen1"):
+        lax.fori_loop(tiles // 2, tiles, widen, 0)
 
     def group(j):
-        return pl.ds(pl.multiple_of(order[j] * pair, pair), pair)
+        if j < nz - 1:
+            return pl.ds(pl.multiple_of(order[j] * pair, pair), pair)
+        side = y if j == nz - 1 else 1 - y
+        return pl.ds(pl.multiple_of((2 * order[nz - 1] + side) * block, block), block)
 
     def quarter(q):
         return pl.ds(pl.multiple_of(q * own_rows, own_rows), own_rows)
@@ -311,7 +358,9 @@
         )
 
     def contract(j):
-        wait_block(1, 2 * order[j] + 1 - y)
+        if j != nz - 1:
+            with jax.named_scope(f"wait_w2y_{j}"):
+                wait_block(1, 2 * order[min(j, nz - 1)] + 1 - y)
         weight = w2_full[group(j), :]
         for t in range(n_mp):
             r = pl.ds(t * own_rows, own_rows)
@@ -333,18 +382,17 @@
             + core_in[g, quarter(my_side)].astype(jnp.float32)
         )
 
-    for j in range(nz):
-        if j + 1 < nz and j >= 1:
-            pass_on(1, j + 1)
+    for j in range(3, nz):
+        with jax.named_scope(f"pass_w2_{j}"):
+            pass_on(1, j)
+    for j in range(nz + 1):
         contract(j)
-        if j == 0 and nz > 2:
-            pass
-        if j >= 1:
-            meet(j - 1)
-    meet(nz - 1)
-
-    for j in range(nz):
-        cross_copy(j).wait_recv()
+        with jax.named_scope(f"meet_{j}"):
+            meet(j)
+
+    for j in range(nz + 1):
+        with jax.named_scope(f"wait_x_{j}"):
+            cross_copy(j).wait_recv()
         final[group(j), :] = final[group(j), :] + cross_in[group(j), :].astype(jnp.float32)
 
     value = final[...]
@@ -363,8 +411,8 @@
         pooled = jnp.where(row_place == image, one, pooled)
     image_emb = unit_vector(pooled * gain_ref[1:2, :])
 
-    for k in range(1, n_dp):
-        text_copy(k).wait_recv()
+    for j in range(nz):
+        wait_block(2, 2 * order[j] + 1 - y)
     every_text = texts[...].astype(jnp.float32).reshape(pairs, width)
     every_text = jnp.concatenate([every_text, jnp.zeros((LANES - pairs, width), jnp.float32)], axis=0)
     scores = sharp_ref[0] * dot_nt(image_emb, every_text.astype(jnp.bfloat16)) + offset_ref[0]
@@ -398,26 +446,26 @@
 
     lax.fori_loop(1, n_all, send_msg, 0)
 
-    for w in range(2):
-        @pl.when(z + 1 < nz)
-        def _():
-            own_z_copy(w, 1).wait_send()
-
-        @pl.when(z >= 1)
-        def _():
-            own_z_copy(w, -1).wait_send()
-
-        for j in range(nz):
-            y_copy(w, j).wait_send()
-            if j >= 1:
-
-                @pl.when(can_pass(j))
-                def _():
-                    pass_on_copy(w, j).wait_send()
-
-    for k in range(1, n_dp):
-        text_copy(k).wait_send()
-    for j in range(nz):
+    for w in range(3):
+        for c in range(counts[w]):
+
+            @pl.when(z + 1 < nz)
+            def _():
+                own_z_copy(w, 1, c).wait_send()
+
+            @pl.when(z >= 1)
+            def _():
+                own_z_copy(w, -1, c).wait_send()
+
+            for j in range(nz):
+                y_copy(w, j, c).wait_send()
+                if j >= 1:
+
+                    @pl.when(can_pass(j))
+                    def _():
+                        pass_on_copy(w, j, c).wait_send()
+
+    for j in range(nz + 1):
         for s in range(sides_x):
             core_copy(j, s).wait_send()
         cross_copy(j).wait_send()
@@ -426,7 +474,8 @@
         msg_copy(k).wait()
         return carry
 
-    lax.fori_loop(1, n_all, end_msg, 0)
+    with jax.named_scope("end_msg"):
+        lax.fori_loop(1, n_all, end_msg, 0)
 
     total = jnp.zeros((1, LANES), jnp.float32)
     for s in range(n_all):
@@ -446,7 +495,8 @@
             jnp.logical_and(wide_r >= pairs, wide_r < pairs + own_images),
         )
         row_own = row_own + jnp.sum(jnp.where(mine, theirs, 0.0), axis=1, keepdims=True)
-    out_ref[...] = jnp.where(wide == 0, row_own, col_own)
+    out_ref[0:1, :] = jnp.sum(jnp.where(place_r == wide_r, row_own, 0.0), axis=0, keepdims=True)[:, :dev_images]
+    out_ref[1:2, :] = jnp.sum(jnp.where(place == wide, col_own, 0.0), axis=0, keepdims=True)[:, :dev_texts]
 
 
 def fused(
@@ -463,10 +513,6 @@
 ):
     rows, width = picture_skip_activations.shape
     block, hidden = widening_matrix.shape
-    extra = -hidden % LANES
-    hidden += extra
-    w1 = jnp.pad(widening_matrix, ((0, 0), (0, extra)))
-    w2 = jnp.pad(contracting_matrix, ((0, extra), (0, 0))).T
     own_rows = rows // n_mp
     nz, sides_x, n_all = n_dp // 2, n_mp // 2, n_dp * n_mp
     dev_texts = caption_closing_activations.shape[0]
@@ -477,7 +523,7 @@
     dma = pltpu.SemaphoreType.DMA
     out = pl.pallas_call(
         functools.partial(fused_kernel, n_dp, n_mp),
-        out_shape=jax.ShapeDtypeStruct((dev_texts, LANES), f32),
+        out_shape=jax.ShapeDtypeStruct((2, dev_texts), f32),
         in_specs=[hbm, vmem, vmem, vmem, vmem, hbm, smem, smem],
         out_specs=vmem,
         scratch_shapes=[
@@ -496,15 +542,13 @@
             pltpu.VMEM((1, LANES), f32),
             pltpu.VMEM((n_all, 1, LANES), f32),
             dma((2,)),
-            dma((2, nz)),
-            dma((2, nz + 1)),
-            dma((2, n_dp)),
-            dma((n_dp,)),
-            dma((n_dp,)),
-            dma((nz, sides_x)),
-            dma((nz, sides_x)),
-            dma((nz,)),
-            dma((nz,)),
+            dma((3, nz, 3)),
+            dma((3, nz + 1, 3)),
+            dma((3, n_dp, 3)),
+            dma((nz + 1, sides_x)),
+            dma((nz + 1, sides_x)),
+            dma((nz + 1,)),
+            dma((nz + 1,)),
             dma((n_all,)),
             dma((n_all,)),
         ],
@@ -515,13 +559,13 @@
         picture_skip_activations,
         caption_closing_activations,
         normaliser_multipliers,
-        w1,
-        w2,
+        widening_matrix,
+        contracting_matrix.T,
         caption_mapping_matrix,
         sharpness_factor,
         score_offset_term,
     )
-    return out[:, 0], out[:, 1]
+    return out[0], out[1]
 
 
 def pick(n_dp, n_mp, *args):

time: 101 us -> 99.8 us (0.988)
  local copies, waits for them, and re-layouts: 4.92 us -> 1.25 us
  Pallas kernels: 93.9 us -> 96.5 us
    pallas_call x1, Pallas kernels: 93.9 us -> 96.5 us  [fused(): pl.pallas_call(functools.partial(fused_kernel, n_dp, n_mp), out_shape=jax...]
    transpose x1 -> x0, local copies, waits for them, and re-layouts: 1.73 us -> none  [fused(): w2 = jnp.pad(contracting_matrix, ((0, extra), (0, 0))).T]
    pad x1 -> x0, local copies, waits for them, and re-layouts: 1.71 us -> none  [fused(): w1 = jnp.pad(widening_matrix, ((0, 0), (0, extra)))]
    slice x1 -> x0, local copies, waits for them, and re-layouts: 1.47 us -> none  [fused(): return (out[:, 0], out[:, 1])]
    squeeze x0 -> x1, local copies, waits for them, and re-layouts: none -> 1.25 us  [fused(): return (out[0], out[1])]
where the time goes in v2:
time: 99.8 us; the launch traced here: 99.7 us
  Pallas kernels  96.5 us (97%)
  between operations  1.93 us (2%)
  local copies, waits for them, and re-layouts  1.25 us (1%)
    pallas_call x1, Pallas kernels, fused(): pl.pallas_call(functools.partial(fused_kernel, n_dp, n_mp), out_shape=jax...  96.5 us

profile of v2, /device:TPU:0, one launch (start us, length us, event | category | flops | bytes accessed | tf_op | source)
XLA Modules:
  0.0 99.7 jit_solution(1661092088215870991)
XLA Ops:
  1.9 96.5 %shard_map.95 = f32[2,8]{1,0:T(2,128)} custom-call(bf16[2048,1152]{1,0:T(8,128)(2,1)} %x_hbm.1, bf16[8,1152]{1,0:T(8,128)(2,1)} %text_ref.1, f32[3,1152]{1,0:T(4,128)} %gain_ref.1, bf16[144,1076]{1,0:T(8,128)(2,1)} %w1_own.1, bf16[144,1076]{1,0:T(8,128)(2,1)} %bitcast.5, bf16[1152,1152]{1,0:T(8,128)(2,1)} %map_hbm.1, f32[1]{0:T(128)S(6)} %copy.10.sharp_ref, ...), custom_call_target="tpu_custom_call" | custom-call | tf_op jit(solution)/shard_map/pallas_call | solution.py:524
  98.4 1.3 %slice_bitcast_fusion = (f32[8]{0:T(128)}, f32[8]{0:T(128)}) fusion(f32[2,8]{1,0:T(2,128)} %shard_map.95), kind=kLoop, calls=%fused_computation | loop fusion | bytes 128 | tf_op jit(solution)/shard_map/squeeze | solution.py:568
